TPU v7x, 32 devices: a whole 2x2x4 slice. The times are simulated.
32 devices in a mesh: seq: 8 (over z, y), chan: 4 (over x, core).
Axes of the slice: x: 2, y: 2, z: 4, core: 2. Of those that a mesh axis runs over, the one named last changes fastest.
Arguments:
- hidden_in: bfloat16 [1024, 2048], P('seq', 'chan'), may hold values from -6 to 6
- norm_gain: float32 [2048], replicated, may hold values from 0.5 to 1.5
- in_weight: bfloat16 [2048, 2, 4096], P('seq', None, 'chan'), may hold values from -0.125 to 0.125
- conv_weight: float32 [2, 4, 4096], P(None, None, 'chan'), may hold values from -3 to 3
- conv_bias: float32 [2, 4096], P(None, 'chan'), may hold values from -0.5 to 0.5
- proj_weight: bfloat16 [2, 4096, 160], P(None, 'chan'), may hold values from -0.1875 to 0.1875
- step_weight: bfloat16 [2, 128, 4096], P(None, None, 'chan'), may hold values from -0.5 to 0.5
- decay_rate: float32 [2, 4096], P(None, 'chan'), may hold values from 0.00024414062 to 0.25
- skip_gain: float32 [2, 4096], P(None, 'chan'), may hold values from 0.5 to 1.5
- out_weight: bfloat16 [4096, 2048], P('chan', 'seq'), may hold values from -0.09375 to 0.09375
Outputs:
- mixed: bfloat16 [1024, 2048], P('seq', 'chan')
All inputs are finite; a program needn't handle non-finite values.
Results may differ from a plain program's by a relative error of at most 0.0095.
Values may be sent and summed in bfloat16 or wider, within the bound.
No kernel may reach another device: no remote copies, remote signals or barrier semaphores. Data moves between devices by JAX's collectives and lax.ppermute only.
A program may use at most 128 MiB of HBM per device.

v0:
```python
import jax
import jax.numpy as jnp
from jax import lax
from jax.sharding import PartitionSpec as P

STATE = 16
WIDTH = 4


def with_halo(block, sides, width):
    for axis, dim in sides:
        count = lax.axis_size(axis)
        forward = [(i, i + 1) for i in range(count - 1)]
        backward = [(target, source) for source, target in forward]
        low = lax.ppermute(
            lax.slice_in_dim(block, block.shape[dim] - width, None, axis=dim), axis, forward
        )
        high = lax.ppermute(lax.slice_in_dim(block, 0, width, axis=dim), axis, backward)
        block = jnp.concatenate([low, block, high], axis=dim)
    return block


def entering(array, axis, combine, identity, reverse):
    devices, here = (lax.axis_size(axis), lax.axis_index(axis))
    everything = jax.tree.map(lambda part: lax.all_gather(part, axis), array)
    start = jax.tree.map(
        lambda part, zero: jnp.broadcast_to(jnp.asarray(zero, part.dtype), part.shape),
        array,
        identity,
    )

    def hop(k, before):
        at = devices - 1 - k if reverse else k
        reached = at > here if reverse else at < here
        new = combine(before, jax.tree.map(lambda part: part[at], everything))
        return jax.tree.map(lambda a, b: jnp.where(reached, a, b), new, before)

    return lax.fori_loop(0, devices, hop, start)


def conv_taps(padded, conv_weight, conv_bias, length):
    reach = conv_weight.shape[1] - 1
    forward = jnp.zeros((length, padded.shape[1]), jnp.float32) + conv_bias[0][None, :]
    backward = jnp.zeros((length, padded.shape[1]), jnp.float32) + conv_bias[1][None, :]
    for offset in range(reach + 1):
        forward = forward + conv_weight[0, offset][None, :] * padded[offset : offset + length]
        begin = 2 * reach - offset
        backward = backward + conv_weight[1, offset][None, :] * padded[begin : begin + length]
    return jax.nn.silu(jnp.stack([forward, backward])).astype(jnp.bfloat16)


def sweep(drive_values, key_rows, query_rows, epsilon, initial, reverse, keeping):
    product = jnp.ones(initial.shape, jnp.float32)

    def advance(carry, current):
        product, state = carry
        drive_row, key_row, query_row, eps_row = current
        decay = 1.0 - eps_row[None, :] * (key_row * key_row)[:, None]
        state = decay * state + key_row[:, None] * (eps_row * drive_row)[None, :]
        product = decay * product
        if keeping == "reads":
            output = jnp.sum(query_row[:, None] * state, axis=0)
        else:
            output = None
        return ((product, state), output)

    (product, state), outputs = lax.scan(
        advance,
        (product, initial),
        (drive_values, key_rows, query_rows, epsilon),
        reverse=reverse,
        unroll=16,
    )
    return (product, state, outputs)


def combine(earlier, latter):
    return (latter[0] * earlier[0], latter[0] * earlier[1] + latter[1])


def per_device(
    hidden_in,
    norm_gain,
    in_weight,
    conv_weight,
    conv_bias,
    proj_weight,
    step_weight,
    decay_rate,
    skip_gain,
    out_weight,
):
    gathered = lax.all_gather(hidden_in, "chan", axis=1, tiled=True).astype(jnp.float32)
    normed = (
        gathered
        * lax.rsqrt(jnp.mean(gathered * gathered, axis=1, keepdims=True) + 1e-05)
        * norm_gain[None, :]
    ).astype(jnp.bfloat16)
    row_count = normed.shape[0]
    channels = in_weight.shape[2]
    piece = lax.all_gather(in_weight, "seq", axis=0, tiled=True)
    projected = jnp.dot(
        normed, piece.reshape(piece.shape[0], 2 * channels), preferred_element_type=jnp.float32
    )
    projected = projected.astype(jnp.bfloat16).reshape(row_count, 2, channels)
    branch = projected[:, 0, :]
    gate_half = projected[:, 1, :].astype(jnp.float32)
    padded = with_halo(branch, (("seq", 0),), WIDTH - 1).astype(jnp.float32)
    driven = conv_taps(padded, conv_weight, conv_bias, row_count)
    partial_value = jnp.einsum(
        "dte,def->tdf", driven, proj_weight, preferred_element_type=jnp.float32
    )
    features = lax.psum(partial_value, "chan")
    key_rows = features[:, :, :STATE]
    query_rows = features[:, :, STATE : 2 * STATE]
    low_rank = features[:, :, 2 * STATE :].astype(jnp.bfloat16)
    step_size = jnp.einsum(
        "tdr,dre->tde", low_rank, step_weight, preferred_element_type=jnp.float32
    )
    beta_rows = 2.0 * decay_rate[None, :, :] * jax.nn.sigmoid(step_size)
    epsilon = beta_rows / (1.0 + beta_rows * jnp.sum(key_rows * key_rows, axis=2, keepdims=True))
    drive_values = driven.astype(jnp.float32)
    zero_state = jnp.zeros((STATE, channels), jnp.float32)
    keeping = "summary"
    passes = [
        sweep(
            drive_values[direction],
            key_rows[:, direction],
            query_rows[:, direction],
            epsilon[:, direction],
            zero_state,
            direction == 1,
            keeping,
        )
        for direction in range(2)
    ]
    identity = (jnp.ones((STATE, channels), jnp.float32), zero_state)
    incoming_forward = entering((passes[0][0], passes[0][1]), "seq", combine, identity, False)[1]
    incoming_reverse = entering((passes[1][0], passes[1][1]), "seq", combine, identity, True)[1]
    incoming = [incoming_forward, incoming_reverse]
    total = jnp.zeros((row_count, channels), jnp.float32)
    for direction in range(2):
        reads = sweep(
            drive_values[direction],
            key_rows[:, direction],
            query_rows[:, direction],
            epsilon[:, direction],
            incoming[direction],
            direction == 1,
            "reads",
        )[2]
        total = total + reads + skip_gain[direction][None, :] * drive_values[direction]
    combined = (total * jax.nn.silu(gate_half)).astype(jnp.bfloat16)
    partial_out = jnp.dot(
        combined,
        lax.all_gather(out_weight, "seq", axis=1, tiled=True),
        preferred_element_type=jnp.float32,
    )
    summed = lax.psum(partial_out, "chan")
    share_width = summed.shape[1] // lax.axis_size("chan")
    share = lax.dynamic_slice_in_dim(summed, lax.axis_index("chan") * share_width, share_width, 1)
    return share.astype(jnp.bfloat16)


def solution(mesh):
    in_specs = (
        P("seq", "chan"),
        P(),
        P("seq", None, "chan"),
        P(None, None, "chan"),
        P(None, "chan"),
        P(None, "chan", None),
        P(None, None, "chan"),
        P(None, "chan"),
        P(None, "chan"),
        P("chan", "seq"),
    )
    out_specs = P("seq", "chan")
    return jax.shard_map(
        per_device, mesh=mesh, in_specs=in_specs, out_specs=out_specs, check_vma=False
    )
```

profile of v0, /device:TPU:0, one launch (start us, length us, event | category | flops | bytes accessed | tf_op | source)
XLA Modules:
  0.0 489.7 jit_solution(10717089666315897083)
XLA Ops:
  7.3 8.9 %all_gather.33 = bf16[128,2048]{1,0:T(8,128)(2,1)S(1)} all-gather(bf16[128,512]{1,0:T(8,128)(2,1)} %param.22), channel_id=1, replica_groups=mesh['seq'=8,'chan'=4] {'chan'}, dimensions={1}, use_global_device_ids=true | all-gather | bytes 655360 | tf_op jit(solution)/shard_map/all_gather | solution.py:93
  17.2 0.9 fusion.339
  18.1 118.6 %all-gather.7.cloned.1.call-done = bf16[2048,2,1024]{2,1,0:T(2,128)(2,1)} async-done(((bf16[256,2,1024]{2,1,0:T(2,128)(2,1)}), bf16[2048,2,1024]{2,1,0:T(2,128)(2,1)}) %all-gather.7.cloned.1.call-update) | async-done | bytes 8388624 | tf_op jit(solution)/shard_map/all_gather | solution.py:101
  136.7 10.1 %copy.42 = bf16[256,8,2,1024]{3,1,2,0:T(8,128)(2,1)} copy(bf16[256,8,2,1024]{3,2,1,0:T(2,128)(2,1)} %bitcast.855) | data formatting | bytes 16777216
  146.8 4.7 convolution_convert_fusion
  152.0 1.3 collective-permute-start.1
  153.3 4.5 collective-permute-start
  157.8 1.5 fusion.335
  160.3 1.0 convolution_bitcast_fusion
  162.2 0.9 fusion.336
  163.2 30.7 %all-reduce.3.cloned.1.call-done = f32[128,2,160]{0,2,1:T(8,128)} async-done(((f32[128,2,160]{0,2,1:T(8,128)}), f32[128,2,160]{0,2,1:T(8,128)}) %all-reduce.3.cloned.1.call-update) | async-done | bytes 163856 | tf_op jit(solution)/shard_map/psum | solution.py:113
  196.4 1.7 add_divide_fusion
  199.1 22.7 %while.92 = (s32[]{:T(128)}, f32[16,1024]{1,0:T(8,128)S(1)}, f32[16,1024]{1,0:T(8,128)S(1)}, f32[8,16,1024]{2,1,0:T(8,128)}, f32[8,16,16]{2,1,0:T(8,128)S(1)}, /...) while((s32[]{:T(128)}, f32[16,1024]{1,0:T(8,128)S(1)}, ...), condition=%wide.region_26.27_spmd.clone, body=%wide.region_25.26_spmd.clone.sunk | while | flops 2146579 | bytes 924200 | solution.py:67
  199.1 2.0 constant_dynamic-slice_fusion.231
  202.1 2.0 constant_dynamic-slice_fusion.231
  205.1 1.8 constant_dynamic-slice_fusion.231
  207.8 1.8 constant_dynamic-slice_fusion.231
  210.6 2.0 constant_dynamic-slice_fusion.231
  213.5 2.0 constant_dynamic-slice_fusion.231
  216.5 1.8 constant_dynamic-slice_fusion.231
  219.2 1.8 constant_dynamic-slice_fusion.231
  221.8 9.5 %while.90 = (s32[]{:T(128)}, f32[16,1024]{1,0:T(8,128)S(1)}, f32[16,1024]{1,0:T(8,128)S(1)}, f32[8,16,1024]{2,1,0:T(8,128)S(1)}, f32[8,16,16]{2,1,0:T(8,128)S(1)...) while((s32[]{:T(128)}, f32[16,1024]{1,0:T(8,128)S(1)}, ...), condition=%wide.region_4.5_spmd.clone, body=%wide.region_3.4_spmd.clone.sunk | while | flops 2146578 | bytes 924180 | solution.py:67
  231.3 37.0 %all-gather.1 = f32[128,1024]{1,0:T(8,128)} all-gather(f32[16,1024]{1,0:T(8,128)S(1)} %get-tuple-element.566), channel_id=3, replica_groups=mesh['seq'=8,'chan'=4] {'seq'}, dimensions={0}, use_global_device_ids=true | all-gather | bytes 589824 | tf_op jit(solution)/shard_map/all_gather | solution.py:25
  268.3 34.7 %all-gather.3 = f32[128,1024]{1,0:T(8,128)} all-gather(f32[16,1024]{1,0:T(8,128)S(1)} %get-tuple-element.570), channel_id=5, replica_groups=mesh['seq'=8,'chan'=4] {'seq'}, dimensions={0}, use_global_device_ids=true | all-gather | bytes 589824 | tf_op jit(solution)/shard_map/all_gather | solution.py:25
  303.0 33.4 %all-gather = f32[128,1024]{1,0:T(8,128)} all-gather(f32[16,1024]{1,0:T(8,128)S(1)} %get-tuple-element.565), channel_id=2, replica_groups=mesh['seq'=8,'chan'=4] {'seq'}, dimensions={0}, use_global_device_ids=true | all-gather | bytes 589824 | tf_op jit(solution)/shard_map/all_gather | solution.py:25
  336.4 7.5 %while.91 = (s32[]{:T(128)}, f32[16,1024]{1,0:T(8,128)S(1)}, s32[]{:T(128)}, f32[8,16,1024]{2,1,0:T(8,128)}, f32[8,16,1024]{2,1,0:T(8,128)}, /*index=5*/s32[]{:T(128)}, s32[]{:T(128)}) while((s32[]{:T(128)}, f32[16,1024]{1,0:T(8,128)S(1)}, s32[]{:T(128)}, f32[8,16,1024]{2,1,0:T(8,128)}, f32[8,16,1024]{2,1,0:T(8,128)}, ...), condition=%wide.region_6.7_spmd.clone, body=%wide.region_5.6_spmd.clone.sunk | while | flops 65540 | bytes 262253 | solution.py:38
  343.9 33.6 %all-gather.2 = f32[128,1024]{1,0:T(8,128)} all-gather(f32[16,1024]{1,0:T(8,128)S(1)} %get-tuple-element.569), channel_id=4, replica_groups=mesh['seq'=8,'chan'=4] {'seq'}, dimensions={0}, use_global_device_ids=true | all-gather | bytes 589824 | tf_op jit(solution)/shard_map/all_gather | solution.py:25
  377.5 7.5 %while.93 = (s32[]{:T(128)}, f32[16,1024]{1,0:T(8,128)S(1)}, s32[]{:T(128)}, f32[8,16,1024]{2,1,0:T(8,128)}, f32[8,16,1024]{2,1,0:T(8,128)}, /*index=5*/s32[]{:T(128)}, s32[]{:T(128)}, s32[]{:T(128)}, s32[]{:T(128)}) while((s32[]{:T(128)}, f32[16,1024]{1,0:T(8,128)S(1)}, s32[]{:T(128)}, f32[8,16,1024]{2,1,0:T(8,128)}, ...), condition=%wide.region_28.29_spmd.clone, body=%wide.region_27.28_spmd.clone.sunk | while | flops 65544 | bytes 262315 | solution.py:38
  378.4 0.9 fusion.368
  379.4 0.9 fusion.368
  380.3 0.9 fusion.368
  381.2 0.9 fusion.368
  382.2 0.9 fusion.368
  383.1 0.9 fusion.368
  384.1 0.9 fusion.368
  385.9 33.0 %while.89 = (s32[]{:T(128)}, f32[16,1024]{1,0:T(8,128)S(1)}, f32[8,16,1024]{2,1,0:T(8,128)}, f32[8,16,1024]{2,1,0:T(8,128)}, f32[8,16,16]{2,1,0:T(8,128)S(1)}, /...) while((s32[]{:T(128)}, f32[16,1024]{1,0:T(8,128)S(1)}, ...), condition=%wide.region_46.47_spmd, body=%wide.region_29.46_spmd.sunk | while | flops 2408722 | bytes 2033121 | solution.py:67
  386.1 2.0 constant_dynamic-slice_fusion.229
  390.3 2.0 constant_dynamic-slice_fusion.229
  394.6 1.8 constant_dynamic-slice_fusion.229
  398.6 1.8 constant_dynamic-slice_fusion.229
  402.6 2.0 constant_dynamic-slice_fusion.229
  406.8 2.0 constant_dynamic-slice_fusion.229
  411.0 1.8 constant_dynamic-slice_fusion.229
  415.0 1.8 constant_dynamic-slice_fusion.229
  418.9 32.4 %while.88 = (s32[]{:T(128)}, f32[16,1024]{1,0:T(8,128)S(1)}, f32[8,16,1024]{2,1,0:T(8,128)S(1)}, f32[8,16,1024]{2,1,0:T(8,128)S(1)}, f32[8,16,16]{2,1,0:T(8,128)...) while((s32[]{:T(128)}, f32[16,1024]{1,0:T(8,128)S(1)}, ...), condition=%wide.region_24.25_spmd, body=%wide.region_7.24_spmd.sunk | while | flops 2490641 | bytes 2106965 | solution.py:67
  418.9 1.1 fusion.359
  420.0 1.1 fusion.360
  423.0 1.0 fusion.359
  424.0 1.1 fusion.360
  427.0 1.0 fusion.359
  428.0 1.1 fusion.360
  431.0 1.1 fusion.359
  432.1 1.1 fusion.360
  435.1 1.1 fusion.359
  436.1 1.1 fusion.360
  439.1 1.0 fusion.359
  440.2 1.1 fusion.360
  443.2 1.0 fusion.359
  444.2 1.1 fusion.360
  447.2 1.1 fusion.359
  448.3 1.1 fusion.360
  451.3 1.5 fusion.203
  452.8 2.9 fusion.342
  455.7 26.7 %all-reduce.4 = bf16[128,2048]{1,0:T(8,128)(2,1)S(1)} all-reduce(f32[128,2048]{1,0:T(8,128)S(1)} %fusion.342), channel_id=1, replica_groups=mesh['seq'=8,'chan'=4] {'chan'}, use_global_device_ids=true, to_apply=%region_47.48 | all-reduce | flops 262144 | bytes 1572864 | tf_op jit(solution)/shard_map/psum | solution.py:159
  (821 shorter events, 61.1 us)
Async XLA Ops:
  6.5 153.8 %copy-start = (bf16[2,1024,160]{1,2,0:T(8,128)(2,1)S(1)}, bf16[2,1024,160]{1,2,0:T(8,128)(2,1)}, u32[]{:S(2)}) copy-start(bf16[2,1024,160]{1,2,0:T(8,128)(2,1)} %param.27) | copy-start | bytes 1966084
  6.5 130.2 %all-gather.7.cloned.1.call-start = ((), (), s32[]{:S(2)}) async-start(), calls=%async_computation | async-start | bytes 9437184 | tf_op jit(solution)/shard_map/all_gather | solution.py:101
  7.3 186.6 %all-reduce.3.cloned.1.call-start = ((), (), s32[]{:S(2)}) async-start(), calls=%async_computation.1 | async-start | bytes 327680 | tf_op jit(solution)/shard_map/psum | solution.py:113
  136.7 10.1 %copy-start.4 = (f32[2048]{0:T(1024)S(1)}, f32[2048]{0:T(1024)}, u32[]{:S(2)}) copy-start(f32[2048]{0:T(1024)} %param.23) | copy-start | bytes 24580
  151.5 10.6 %copy-start.5 = (f32[2,1024]{1,0:T(2,128)S(1)}, f32[2,1024]{1,0:T(2,128)}, u32[]{:S(2)}) copy-start(f32[2,1024]{1,0:T(2,128)} %param.29) | copy-start | bytes 24580
  151.5 10.7 %copy-start.6 = (f32[2,1024]{1,0:T(2,128)S(1)}, f32[2,1024]{1,0:T(2,128)}, u32[]{:S(2)}) copy-start(f32[2,1024]{1,0:T(2,128)} %param.30) | copy-start | bytes 24580
  152.0 7.5 %collective-permute-start.1 = (bf16[3,1024]{1,0:T(4,128)(2,1)S(1)}, bf16[3,1024]{1,0:T(4,128)(2,1)S(1)}, u32[]{:S(2)}, u32[]{:S(2)}) collective-permute-start(bf16[3,1024]{1,0:T(4,128)(2,1)S(1)} %bitcast.1151), channel_id=1, source_target_pairs={{4,0},{8,4},{12,8},{16,12},{20,16},{24,20},{28,24},{5,1},{9,5},{13... | collective-permute-start | bytes 18440 | tf_op jit(solution)/shard_map/ppermute | solution.py:18
  153.3 6.2 %collective-permute-start = (bf16[3,1024]{1,0:T(4,128)(2,1)S(1)}, bf16[3,1024]{1,0:T(4,128)(2,1)S(1)}, u32[]{:S(2)}, u32[]{:S(2)}) collective-permute-start(bf16[3,1024]{1,0:T(4,128)(2,1)S(1)} %bitcast.1150), channel_id=1, source_target_pairs={{0,4},{4,8},{8,12},{12,16},{16,20},{20,24},{24,28},{1,5},{5,9},{9,... | collective-permute-start | bytes 18440 | tf_op jit(solution)/shard_map/ppermute | solution.py:15
  161.4 291.4 %all-gather.9.cloned.1.call-start = ((), (), s32[]{:S(2)}) async-start(), calls=%async_computation.2 | async-start | bytes 4718592 | tf_op jit(solution)/shard_map/all_gather | solution.py:156
  163.2 35.9 %copy-start.1 = (f32[16,1024]{1,0:T(8,128)S(1)}, f32[16,1024]{1,0:T(8,128)}, u32[]{:S(2)}) copy-start(f32[16,1024]{1,0:T(8,128)} %custom-call.4) | copy-start | bytes 196612
  163.2 35.9 %copy-start.2 = (f32[16,1024]{1,0:T(8,128)S(1)}, f32[16,1024]{1,0:T(8,128)}, u32[]{:S(2)}) copy-start(f32[16,1024]{1,0:T(8,128)} %custom-call.3) | copy-start | bytes 196612
  231.3 154.6 %copy-start.3 = (f32[8,16,16]{2,1,0:T(8,128)}, f32[8,16,16]{2,1,0:T(8,128)S(1)}, u32[]{:S(2)}) copy-start(f32[8,16,16]{2,1,0:T(8,128)S(1)} %get-tuple-element.2563) | copy-start | bytes 24580
Sparse Core Ops, SparseCore 0:
  9.5 127.1 all-gather.6
  161.5 32.3 all-reduce.2
  195.9 86.4 all-gather.8
where the time goes:
time: 494 us; the launch traced here: 490 us
  blocking collectives  174 us (35%)
  waiting for transfers between devices  151 us (31%)
  local copies, waits for them, and re-layouts  69.2 us (14%)
  other arithmetic  59.8 us (12%)
  between operations  13.4 us (3%)
  matrix products  10.3 us (2%)
  loops' own time  6.06 us (1%)
  starting transfers between devices  5.92 us (1%)
    all_gather x4, blocking collectives, entering(): everything = jax.tree.map(lambda part: lax.all_gather(part, axis), array)  139 us
    all_gather x1, waiting for transfers between devices, per_device(): piece = lax.all_gather(in_weight, 'seq', axis=0, tiled=True)  119 us
    slice x32, local copies, waits for them, and re-layouts, sweep(): lax.scan(advance, (product, initial), (drive_values, key_rows, query_rows...  34.3 us
    psum x1, waiting for transfers between devices, per_device(): features = lax.psum(partial_value, 'chan')  30.7 us
    psum x1, blocking collectives, per_device(): summed = lax.psum(partial_out, 'chan')  26.7 us
    reduce_sum x136, other arithmetic, advance(): output = jnp.sum(query_row[:, None] * state, axis=0)  17.7 us
    select_n x16, other arithmetic, hop(): return jax.tree.map(lambda a, b: jnp.where(reached, a, b), new, before)  14.6 us
    mul x32, other arithmetic, advance(): decay = 1.0 - eps_row[None, :] * (key_row * key_row)[:, None]  12.7 us
  transfers between devices with their start and end apart: 5, of which 2 were waited for; matrix products, arithmetic and copies ran while one was open for 24% of the time, Pallas kernels for 0%

commit v1 on v0

--- a/solution.py
+++ b/solution.py
@@ -1,3 +1,4 @@
+import functools
 import jax
 import jax.numpy as jnp
 from jax import lax
@@ -5,6 +6,24 @@
 
 STATE = 16
 WIDTH = 4
+
+
+def _touch_knots(w_in, array_dim):
+    n_axis = lax.axis_size("seq")
+    local_part = sorted(((u, (u + 1) % n_axis) for u in range(n_axis)))
+    val2 = w_in
+    seen = [val2]
+    for d in range(1, n_axis):
+        val2 = lax.ppermute(val2, "seq", local_part)
+        seen.insert(0, val2)
+    current_value = jnp.concatenate(seen, array_dim)
+    w1 = lax.axis_index("seq")
+    built = w1 + 1
+    r_now = jnp.roll(current_value, built * w_in.shape[array_dim], array_dim)
+    return r_now
+
+
+press_targets_in = functools.partial(_touch_knots, array_dim=0)
 
 
 def with_halo(block, sides, width):
@@ -98,7 +117,7 @@
     ).astype(jnp.bfloat16)
     row_count = normed.shape[0]
     channels = in_weight.shape[2]
-    piece = lax.all_gather(in_weight, "seq", axis=0, tiled=True)
+    piece = press_targets_in(in_weight)
     projected = jnp.dot(
         normed, piece.reshape(piece.shape[0], 2 * channels), preferred_element_type=jnp.float32
     )

time: 494 us -> 597 us (1.21)
  waiting for transfers between devices: 151 us -> 197 us
  local copies, waits for them, and re-layouts: 69.2 us -> 106 us
  other arithmetic: 59.8 us -> 88.6 us
  blocking collectives: 174 us -> 163 us
    ppermute x0 -> x7, waiting for transfers between devices: none -> 167 us  [_touch_knots(): val2 = lax.ppermute(val2, 'seq', local_part)]
    all_gather x1 -> x0, waiting for transfers between devices: 119 us -> none  [per_device(): piece = lax.all_gather(in_weight, 'seq', axis=0, tiled=True)]
    unnamed x20 -> x55, local copies, waits for them, and re-layouts: 10.5 us -> 38.6 us
    add x16, other arithmetic: 5.87 us -> 16.8 us  [advance(): state = decay * state + key_row[:, None] * (eps_row * drive_row)[None, :]]
    mul x16, other arithmetic: 3.1 us -> 13.8 us  [advance(): product = decay * product]
    all_gather x4, blocking collectives: 139 us -> 131 us  [entering(): everything = jax.tree.map(lambda part: lax.all_gather(part, axis), array)]
    mul x32, other arithmetic: 12.7 us -> 20.4 us  [advance(): decay = 1.0 - eps_row[None, :] * (key_row * key_row)[:, None]]
    dynamic_slice x0 -> x1, local copies, waits for them, and re-layouts: none -> 7.02 us  [_touch_knots(): r_now = jnp.roll(current_value, built * w_in.shape[array_dim], array_dim)]
  transfers between devices with their start and end apart: 5 -> 11, of which waited for: 2 -> 9; matrix products, arithmetic and copies ran while one was open for 24% -> 25% of each run, Pallas kernels for 0% -> 0%
where the time goes in v1:
time: 597 us; the launch traced here: 591 us
  waiting for transfers between devices  197 us (33%)
  blocking collectives  163 us (27%)
  local copies, waits for them, and re-layouts  106 us (18%)
  other arithmetic  88.6 us (15%)
  between operations  15.2 us (3%)
  matrix products  10.4 us (2%)
    ppermute x7, waiting for transfers between devices, _touch_knots(): val2 = lax.ppermute(val2, 'seq', local_part)  167 us
    all_gather x4, blocking collectives, entering(): everything = jax.tree.map(lambda part: lax.all_gather(part, axis), array)  131 us
    unnamed x55, local copies, waits for them, and re-layouts  38.6 us
    slice x32, local copies, waits for them, and re-layouts, sweep(): lax.scan(advance, (product, initial), (drive_values, key_rows, query_rows...  32.4 us
    psum x1, waiting for transfers between devices, per_device(): features = lax.psum(partial_value, 'chan')  26.4 us
    psum x1, blocking collectives, per_device(): summed = lax.psum(partial_out, 'chan')  25.2 us
    mul x32, other arithmetic, advance(): decay = 1.0 - eps_row[None, :] * (key_row * key_row)[:, None]  20.4 us
    reduce_sum x136, other arithmetic, advance(): output = jnp.sum(query_row[:, None] * state, axis=0)  17.7 us
  transfers between devices with their start and end apart: 11, of which 9 were waited for; matrix products, arithmetic and copies ran while one was open for 25% of the time, Pallas kernels for 0%

profile of v1, /device:TPU:0, one launch (start us, length us, event | category | flops | bytes accessed | tf_op | source)
XLA Modules:
  0.0 591.0 jit_solution(3899246912004150065)
XLA Ops:
  7.4 3.0 collective-permute-start
  10.4 26.4 %collective-permute-done = bf16[256,2,1024]{2,1,0:T(2,128)(2,1)S(1)} collective-permute-done((bf16[256,2,1024]{2,1,0:T(2,128)(2,1)}, bf16[256,2,1024]{2,1,0:T(2,128)(2,1)S(1)}, u32[]{:S(2)}, u32[]{:S(2)}) %collective-permute-start) | collective-permute-done | bytes 1048608 | tf_op jit(solution)/shard_map/ppermute | solution.py:17
  36.8 27.0 %collective-permute-done.1 = bf16[256,2,1024]{2,1,0:T(2,128)(2,1)S(1)} collective-permute-done((bf16[256,2,1024]{2,1,0:T(2,128)(2,1)S(1)}, bf16[256,2,1024]{2,1,0:T(2,128)(2,1)S(1)}, u32[]{:S(2)}, u32[]{:S(2)}) %collective-permute-start.1) | collective-permute-done | bytes 1048608 | tf_op jit(solution)/shard_map/ppermute | solution.py:17
  64.8 26.2 %collective-permute-done.2 = bf16[256,2,1024]{2,1,0:T(2,128)(2,1)S(1)} collective-permute-done((bf16[256,2,1024]{2,1,0:T(2,128)(2,1)S(1)}, bf16[256,2,1024]{2,1,0:T(2,128)(2,1)S(1)}, u32[]{:S(2)}, u32[]{:S(2)}) %collective-permute-start.2) | collective-permute-done | bytes 1048608 | tf_op jit(solution)/shard_map/ppermute | solution.py:17
  92.0 25.3 %collective-permute-done.3 = bf16[256,2,1024]{2,1,0:T(2,128)(2,1)S(1)} collective-permute-done((bf16[256,2,1024]{2,1,0:T(2,128)(2,1)S(1)}, bf16[256,2,1024]{2,1,0:T(2,128)(2,1)S(1)}, u32[]{:S(2)}, u32[]{:S(2)}) %collective-permute-start.3) | collective-permute-done | bytes 1048608 | tf_op jit(solution)/shard_map/ppermute | solution.py:17
  118.3 24.4 %collective-permute-done.4 = bf16[256,2,1024]{2,1,0:T(2,128)(2,1)S(1)} collective-permute-done((bf16[256,2,1024]{2,1,0:T(2,128)(2,1)S(1)}, bf16[256,2,1024]{2,1,0:T(2,128)(2,1)S(1)}, u32[]{:S(2)}, u32[]{:S(2)}) %collective-permute-start.4) | collective-permute-done | bytes 1048608 | tf_op jit(solution)/shard_map/ppermute | solution.py:17
  143.7 23.7 %collective-permute-done.5 = bf16[256,2,1024]{2,1,0:T(2,128)(2,1)} collective-permute-done((bf16[256,2,1024]{2,1,0:T(2,128)(2,1)S(1)}, bf16[256,2,1024]{2,1,0:T(2,128)(2,1)}, u32[]{:S(2)}, u32[]{:S(2)}) %collective-permute-start.5) | collective-permute-done | bytes 1048608 | tf_op jit(solution)/shard_map/ppermute | solution.py:17
  167.5 6.8 %all_gather.30 = bf16[128,2048]{1,0:T(8,128)(2,1)S(1)} all-gather(bf16[128,512]{1,0:T(8,128)(2,1)} %param.22), channel_id=1, replica_groups=mesh['seq'=8,'chan'=4] {'chan'}, dimensions={1}, use_global_device_ids=true | all-gather | bytes 655360 | tf_op jit(solution)/shard_map/all_gather | solution.py:112
  176.3 14.2 %collective-permute-done.6 = bf16[256,2,1024]{2,1,0:T(2,128)(2,1)} collective-permute-done((bf16[256,2,1024]{2,1,0:T(2,128)(2,1)}, bf16[256,2,1024]{2,1,0:T(2,128)(2,1)}, u32[]{:S(2)}, u32[]{:S(2)}) %collective-permute-start.6) | collective-permute-done | bytes 1048608 | tf_op jit(solution)/shard_map/ppermute | solution.py:17
  190.5 1.9 constant_dynamic-update-slice_fusion.15
  192.5 2.0 constant_dynamic-update-slice_fusion.14
  194.5 2.0 constant_dynamic-update-slice_fusion.13
  196.5 2.0 constant_dynamic-update-slice_fusion.12
  198.5 2.0 constant_dynamic-update-slice_fusion.11
  200.5 2.0 constant_dynamic-update-slice_fusion.10
  203.3 2.0 constant_dynamic-update-slice_fusion.8
  205.3 2.0 constant_dynamic-update-slice_fusion.7
  207.3 2.0 constant_dynamic-update-slice_fusion.6
  214.3 7.0 %constant_dynamic-slice_fusion.224 = bf16[2048,2,1024]{2,1,0:T(2,128)(2,1)} fusion(bf16[4096,2,1024]{2,1,0:T(2,128)(2,1)S(1)} %constant_dynamic-update-slice_fusion, s32[]{:T(128)S(6)} %select_n.70), kind=kLoop, calls=%fused_computation.581 | loop fusion | bytes 16777220 | tf_op jit(solution)/shard_map/jit(_roll_dynamic)/dynamic_slice | solution.py:22
  221.3 10.1 %copy.31 = bf16[256,8,2,1024]{3,1,2,0:T(8,128)(2,1)} copy(bf16[256,8,2,1024]{3,2,1,0:T(2,128)(2,1)} %bitcast.855) | data formatting | bytes 16777216
  231.4 4.7 convolution_convert_fusion
  240.8 2.6 collective-permute-done.8
  247.5 26.4 %all-reduce.3.cloned.1.call-done = f32[128,2,160]{0,2,1:T(8,128)} async-done(((f32[128,2,160]{0,2,1:T(8,128)}), f32[128,2,160]{0,2,1:T(8,128)}) %all-reduce.3.cloned.1.call-update) | async-done | bytes 163856 | tf_op jit(solution)/shard_map/psum | solution.py:132
  274.7 1.7 add_divide_fusion
  278.8 30.2 %while.90 = (s32[]{:T(128)}, f32[16,1024]{1,0:T(8,128)}, f32[16,1024]{1,0:T(8,128)}, f32[8,16,1024]{2,1,0:T(8,128)S(1)}, f32[8,16,16]{2,1,0:T(8,128)S(1)}, /*ind...) while((s32[]{:T(128)}, f32[16,1024]{1,0:T(8,128)}, ...), condition=%wide.region_4.5_spmd.clone, body=%wide.region_3.4_spmd.clone.sunk | while | flops 2146578 | bytes 924172 | solution.py:86
  281.7 1.8 multiply_add_fusion.52
  283.6 1.6 fusion.364
  285.7 1.8 multiply_add_fusion.52
  287.5 1.6 fusion.364
  289.7 1.8 multiply_add_fusion.52
  293.6 1.8 multiply_add_fusion.52
  295.5 1.6 fusion.364
  297.6 1.8 multiply_add_fusion.52
  299.4 1.6 fusion.364
  301.6 1.8 multiply_add_fusion.52
  305.5 1.8 multiply_add_fusion.52
  307.4 1.6 fusion.364
  309.6 32.3 %all-gather = f32[128,1024]{1,0:T(8,128)S(1)} all-gather(f32[16,1024]{1,0:T(8,128)} %get-tuple-element.565), channel_id=2, replica_groups=mesh['seq'=8,'chan'=4] {'seq'}, dimensions={0}, use_global_device_ids=true | all-gather | bytes 589824 | tf_op jit(solution)/shard_map/all_gather | solution.py:44
  341.9 33.6 %all-gather.1 = f32[128,1024]{1,0:T(8,128)} all-gather(f32[16,1024]{1,0:T(8,128)} %get-tuple-element.566), channel_id=3, replica_groups=mesh['seq'=8,'chan'=4] {'seq'}, dimensions={0}, use_global_device_ids=true | all-gather | bytes 589824 | tf_op jit(solution)/shard_map/all_gather | solution.py:44
  375.6 7.2 %while.91 = (s32[]{:T(128)}, f32[16,1024]{1,0:T(8,128)S(1)}, s32[]{:T(128)}, f32[8,16,1024]{2,1,0:T(8,128)S(1)}, f32[8,16,1024]{2,1,0:T(8,128)}, /*index=5*/s32[]{:T(128)}, s32[]{:T(128)}) while((s32[]{:T(128)}, f32[16,1024]{1,0:T(8,128)S(1)}, s32[]{:T(128)}, f32[8,16,1024]{2,1,0:T(8,128)S(1)}, f32[8,16,1024]{2,1,0:T(8,128)}, ...), condition=%wide.region_6.7_spmd.clone, body=%wide.region_5.6_spmd.clone.sunk | while | flops 65540 | bytes 262245 | solution.py:57
  384.3 22.8 %while.92 = (s32[]{:T(128)}, f32[16,1024]{1,0:T(8,128)S(1)}, f32[16,1024]{1,0:T(8,128)S(1)}, f32[8,16,1024]{2,1,0:T(8,128)}, f32[8,16,16]{2,1,0:T(8,128)S(1)}, /...) while((s32[]{:T(128)}, f32[16,1024]{1,0:T(8,128)S(1)}, ...), condition=%wide.region_26.27_spmd.clone, body=%wide.region_25.26_spmd.clone.sunk | while | flops 2146579 | bytes 924192 | solution.py:86
  384.3 2.0 constant_dynamic-slice_fusion.232
  387.3 2.0 constant_dynamic-slice_fusion.232
  390.3 1.8 constant_dynamic-slice_fusion.232
  393.1 1.8 constant_dynamic-slice_fusion.232
  395.9 2.0 constant_dynamic-slice_fusion.232
  398.8 2.0 constant_dynamic-slice_fusion.232
  401.7 1.8 constant_dynamic-slice_fusion.232
  404.5 1.8 constant_dynamic-slice_fusion.232
  407.8 31.5 %all-gather.2 = f32[128,1024]{1,0:T(8,128)S(1)} all-gather(f32[16,1024]{1,0:T(8,128)S(1)} %get-tuple-element.569), channel_id=4, replica_groups=mesh['seq'=8,'chan'=4] {'seq'}, dimensions={0}, use_global_device_ids=true | all-gather | bytes 589824 | tf_op jit(solution)/shard_map/all_gather | solution.py:44
  439.3 33.2 %all-gather.3 = f32[128,1024]{1,0:T(8,128)} all-gather(f32[16,1024]{1,0:T(8,128)S(1)} %get-tuple-element.570), channel_id=5, replica_groups=mesh['seq'=8,'chan'=4] {'seq'}, dimensions={0}, use_global_device_ids=true | all-gather | bytes 589824 | tf_op jit(solution)/shard_map/all_gather | solution.py:44
  472.5 7.3 %while.93 = (s32[]{:T(128)}, f32[16,1024]{1,0:T(8,128)S(1)}, s32[]{:T(128)}, f32[8,16,1024]{2,1,0:T(8,128)S(1)}, f32[8,16,1024]{2,1,0:T(8,128)}, /*index=5*/s32[]{:T(128)}, s32[]{:T(128)}, s32[]{:T(128)}, s32[]{:T(128)}) while((s32[]{:T(128)}, f32[16,1024]{1,0:T(8,128)S(1)}, s32[]{:T(128)}, f32[8,16,1024]{2,1,0:T(8,128)S(1)}, ...), condition=%wide.region_28.29_spmd.clone, body=%wide.region_27.28_spmd.clone.sunk | while | flops 65544 | bytes 262307 | solution.py:57
  480.7 40.1 %while.89 = (s32[]{:T(128)}, f32[16,1024]{1,0:T(8,128)S(1)}, f32[8,16,1024]{2,1,0:T(8,128)}, f32[8,16,1024]{2,1,0:T(8,128)}, f32[8,16,16]{2,1,0:T(8,128)}, /*ind...) while((s32[]{:T(128)}, f32[16,1024]{1,0:T(8,128)S(1)}, ...), condition=%wide.region_46.47_spmd, body=%wide.region_29.46_spmd.sunk | while | flops 2408722 | bytes 2033121 | solution.py:86
  480.7 1.9 constant_dynamic-slice_fusion.230
  485.9 1.9 constant_dynamic-slice_fusion.230
  491.0 1.7 constant_dynamic-slice_fusion.230
  495.9 1.7 constant_dynamic-slice_fusion.230
  500.8 1.9 constant_dynamic-slice_fusion.230
  505.9 1.8 constant_dynamic-slice_fusion.230
  511.0 1.7 constant_dynamic-slice_fusion.230
  515.9 1.7 constant_dynamic-slice_fusion.230
  520.8 32.3 %while.88 = (s32[]{:T(128)}, f32[16,1024]{1,0:T(8,128)S(1)}, f32[8,16,1024]{2,1,0:T(8,128)S(1)}, f32[8,16,1024]{2,1,0:T(8,128)S(1)}, f32[8,16,16]{2,1,0:T(8,128)...) while((s32[]{:T(128)}, f32[16,1024]{1,0:T(8,128)S(1)}, ...), condition=%wide.region_24.25_spmd, body=%wide.region_7.24_spmd.sunk | while | flops 2490641 | bytes 2106957 | solution.py:86
  554.7 2.9 fusion.342
  557.6 25.2 %all-reduce.4 = bf16[128,2048]{1,0:T(8,128)(2,1)S(1)} all-reduce(f32[128,2048]{1,0:T(8,128)S(1)} %fusion.342), channel_id=1, replica_groups=mesh['seq'=8,'chan'=4] {'chan'}, use_global_device_ids=true, to_apply=%region_47.48 | all-reduce | flops 262144 | bytes 1572864 | tf_op jit(solution)/shard_map/psum | solution.py:178
  (869 shorter events, 112.8 us)
Async XLA Ops:
  7.4 236.9 %copy-start = (bf16[2,1024,160]{1,2,0:T(8,128)(2,1)S(1)}, bf16[2,1024,160]{1,2,0:T(8,128)(2,1)}, u32[]{:S(2)}) copy-start(bf16[2,1024,160]{1,2,0:T(8,128)(2,1)} %param.27) | copy-start | bytes 1966084
  7.4 206.1 %copy-start.1 = (bf16[256,2,1024]{2,1,0:T(2,128)(2,1)S(1)}, bf16[256,2,1024]{2,1,0:T(2,128)(2,1)}, u32[]{:S(2)}) copy-start(bf16[256,2,1024]{2,1,0:T(2,128)(2,1)} %param.24) | copy-start | bytes 3145732
  7.4 266.6 %all-reduce.3.cloned.1.call-start = ((), (), s32[]{:S(2)}) async-start(), calls=%async_computation | async-start | bytes 327680 | tf_op jit(solution)/shard_map/psum | solution.py:132
  7.4 29.4 %collective-permute-start = (bf16[256,2,1024]{2,1,0:T(2,128)(2,1)}, bf16[256,2,1024]{2,1,0:T(2,128)(2,1)S(1)}, u32[]{:S(2)}, u32[]{:S(2)}) collective-permute-start(bf16[256,2,1024]{2,1,0:T(2,128)(2,1)} %param.24), channel_id=1, source_target_pairs={{0,4},{4,8},{8,12},{12,16},{16,20},{20,24},{24,28},{28,0},{1,5},{5... | collective-permute-start | bytes 3145736 | tf_op jit(solution)/shard_map/ppermute | solution.py:17
  36.8 27.0 %collective-permute-start.1 = (bf16[256,2,1024]{2,1,0:T(2,128)(2,1)S(1)}, bf16[256,2,1024]{2,1,0:T(2,128)(2,1)S(1)}, u32[]{:S(2)}, u32[]{:S(2)}) collective-permute-start(bf16[256,2,1024]{2,1,0:T(2,128)(2,1)S(1)} %collective-permute-done), channel_id=1, source_target_pairs={{0,4},{4,8},{8,12},{12,16},{16,20},{20,24},{24,28},{28,0},{1,5},{5... | collective-permute-start | bytes 3145736 | tf_op jit(solution)/shard_map/ppermute | solution.py:17
  63.8 1.0 copy-start.2
  64.8 26.2 %collective-permute-start.2 = (bf16[256,2,1024]{2,1,0:T(2,128)(2,1)S(1)}, bf16[256,2,1024]{2,1,0:T(2,128)(2,1)S(1)}, u32[]{:S(2)}, u32[]{:S(2)}) collective-permute-start(bf16[256,2,1024]{2,1,0:T(2,128)(2,1)S(1)} %collective-permute-done.1), channel_id=1, source_target_pairs={{0,4},{4,8},{8,12},{12,16},{16,20},{20,24},{24,28},{28,0},{1,5},{5... | collective-permute-start | bytes 3145736 | tf_op jit(solution)/shard_map/ppermute | solution.py:17
  91.0 1.0 copy-start.4
  92.0 25.3 %collective-permute-start.3 = (bf16[256,2,1024]{2,1,0:T(2,128)(2,1)S(1)}, bf16[256,2,1024]{2,1,0:T(2,128)(2,1)S(1)}, u32[]{:S(2)}, u32[]{:S(2)}) collective-permute-start(bf16[256,2,1024]{2,1,0:T(2,128)(2,1)S(1)} %collective-permute-done.2), channel_id=1, source_target_pairs={{0,4},{4,8},{8,12},{12,16},{16,20},{20,24},{24,28},{28,0},{1,5},{5... | collective-permute-start | bytes 3145736 | tf_op jit(solution)/shard_map/ppermute | solution.py:17
  117.3 1.0 copy-start.6
  118.3 24.5 %collective-permute-start.4 = (bf16[256,2,1024]{2,1,0:T(2,128)(2,1)S(1)}, bf16[256,2,1024]{2,1,0:T(2,128)(2,1)S(1)}, u32[]{:S(2)}, u32[]{:S(2)}) collective-permute-start(bf16[256,2,1024]{2,1,0:T(2,128)(2,1)S(1)} %collective-permute-done.3), channel_id=1, source_target_pairs={{0,4},{4,8},{8,12},{12,16},{16,20},{20,24},{24,28},{28,0},{1,5},{5... | collective-permute-start | bytes 3145736 | tf_op jit(solution)/shard_map/ppermute | solution.py:17
  142.8 1.0 copy-start.8
  143.7 23.7 %collective-permute-start.5 = (bf16[256,2,1024]{2,1,0:T(2,128)(2,1)S(1)}, bf16[256,2,1024]{2,1,0:T(2,128)(2,1)}, u32[]{:S(2)}, u32[]{:S(2)}) collective-permute-start(bf16[256,2,1024]{2,1,0:T(2,128)(2,1)S(1)} %collective-permute-done.4), channel_id=1, source_target_pairs={{0,4},{4,8},{8,12},{12,16},{16,20},{20,24},{24,28},{28,0},{1,5},{5... | collective-permute-start | bytes 3145736 | tf_op jit(solution)/shard_map/ppermute | solution.py:17
  167.4 23.1 %collective-permute-start.6 = (bf16[256,2,1024]{2,1,0:T(2,128)(2,1)}, bf16[256,2,1024]{2,1,0:T(2,128)(2,1)}, u32[]{:S(2)}, u32[]{:S(2)}) collective-permute-start(bf16[256,2,1024]{2,1,0:T(2,128)(2,1)} %collective-permute-done.5), channel_id=1, source_target_pairs={{0,4},{4,8},{8,12},{12,16},{16,20},{20,24},{24,28},{28,0},{1,5},{5... | collective-permute-start | bytes 3145736 | tf_op jit(solution)/shard_map/ppermute | solution.py:17
  167.5 41.8 %copy-start.9 = (bf16[256,2,1024]{2,1,0:T(2,128)(2,1)S(1)}, bf16[256,2,1024]{2,1,0:T(2,128)(2,1)}, u32[]{:S(2)}) copy-start(bf16[256,2,1024]{2,1,0:T(2,128)(2,1)} %copy-done.8) | copy-start | bytes 3145732
  167.5 42.7 %copy-start.7 = (bf16[256,2,1024]{2,1,0:T(2,128)(2,1)S(1)}, bf16[256,2,1024]{2,1,0:T(2,128)(2,1)}, u32[]{:S(2)}) copy-start(bf16[256,2,1024]{2,1,0:T(2,128)(2,1)} %copy-done.6) | copy-start | bytes 3145732
  167.5 43.5 %copy-start.5 = (bf16[256,2,1024]{2,1,0:T(2,128)(2,1)S(1)}, bf16[256,2,1024]{2,1,0:T(2,128)(2,1)}, u32[]{:S(2)}) copy-start(bf16[256,2,1024]{2,1,0:T(2,128)(2,1)} %copy-done.4) | copy-start | bytes 3145732
  167.5 44.3 %copy-start.3 = (bf16[256,2,1024]{2,1,0:T(2,128)(2,1)S(1)}, bf16[256,2,1024]{2,1,0:T(2,128)(2,1)}, u32[]{:S(2)}) copy-start(bf16[256,2,1024]{2,1,0:T(2,128)(2,1)} %copy-done.2) | copy-start | bytes 3145732
  214.3 17.2 %copy-start.12 = (f32[2048]{0:T(1024)S(1)}, f32[2048]{0:T(1024)}, u32[]{:S(2)}) copy-start(f32[2048]{0:T(1024)} %param.23) | copy-start | bytes 24580
  231.4 14.5 %copy-start.15 = (f32[2,1024]{1,0:T(2,128)S(1)}, f32[2,1024]{1,0:T(2,128)}, u32[]{:S(2)}) copy-start(f32[2,1024]{1,0:T(2,128)} %param.29) | copy-start | bytes 24580
  231.4 14.6 %copy-start.16 = (f32[2,1024]{1,0:T(2,128)S(1)}, f32[2,1024]{1,0:T(2,128)}, u32[]{:S(2)}) copy-start(f32[2,1024]{1,0:T(2,128)} %param.30) | copy-start | bytes 24580
  236.6 4.2 collective-permute-start.7
  237.9 5.5 collective-permute-start.8
  245.3 309.4 %all-gather.6.cloned.1.call-start = ((), (), s32[]{:S(2)}) async-start(), calls=%async_computation.1 | async-start | bytes 4718592 | tf_op jit(solution)/shard_map/all_gather | solution.py:175
  309.0 0.6 copy-start.10
  384.3 168.8 %copy-start.13 = (f32[1,1024]{1,0:T(1,128)S(1)}, f32[1,1024]{1,0:T(1,128)}, u32[]{:S(2)}) copy-start(f32[1,1024]{1,0:T(1,128)} %get-tuple-element.1292) | copy-start | bytes 12292
  384.3 168.8 %copy-start.14 = (f32[1,1024]{1,0:T(1,128)S(1)}, f32[1,1024]{1,0:T(1,128)}, u32[]{:S(2)}) copy-start(f32[1,1024]{1,0:T(1,128)} %get-tuple-element.1293) | copy-start | bytes 12292
  407.2 0.6 copy-start.11
Sparse Core Ops, SparseCore 0:
  245.5 28.4 all-reduce.2
Sparse Core Ops, SparseCore 1:
  247.9 72.5 all-gather.5
